TPU v7x, 128 devices: a whole 4x4x4 slice. The times are simulated.
128 devices in a mesh: group: 4 (over x_lo, core), bl: 32 (over x_hi, y, z).
Axes of the slice: x: 4 (x_hi: 2, x_lo: 2; x = x_hi * 2 + x_lo), y: 4, z: 4, core: 2. Of those that a mesh axis runs over, the one named last changes fastest.
Arguments:
- visibilities: float32 [2, 2048, 16, 1024], P(None, ('group', 'bl')), parts along dimension 1, may hold values from -400 to 400
- flags: int32 [2048, 8], P(('group', 'bl')), parts along dimension 0, may hold values 0 or 1
Outputs:
- cross_power: float32 [32, 2048, 512], P(None, ('group', 'bl')), parts along dimension 1
- bandpower: float32 [128], P('group'), parts along dimension 0
There are 4 independent parts, one for each index of `group`. A program takes and returns all parts, laid end to end along the dimension named above; each array names one. Nothing has to cross between parts.
All inputs are finite; a program needn't handle non-finite values. No bound on the sum of `flags` on one device may be relied on, other than what follows from the above.
Results may differ from a plain program's by a relative error of at most 0.004.
Values may be sent and summed in bfloat16 or wider, within the bound.
No kernel may reach another device: no remote copies, remote signals or barrier semaphores. Data moves between devices by JAX's collectives and lax.ppermute only.
A program may use at most 192 MiB of HBM per device.

v0:
```python
import math
import jax
import jax.numpy as jnp
from jax import lax
from jax.sharding import PartitionSpec as P

NF = 1024
NT = 16
CB = 128
BW = 32


def copy_for_each(array, axis):
    copies = jnp.broadcast_to(array, (lax.axis_size(axis), *array.shape))
    return lax.all_to_all(copies, axis, split_axis=0, concat_axis=0, tiled=True)


def taken_together(array, axis):
    return copy_for_each(array, axis).sum(axis=0)


def make_taper():
    angle = jnp.arange(NF, dtype=jnp.int32).astype(jnp.float32) * (2.0 * math.pi / (NF - 1))
    return (
        0.35875
        - 0.48829 * jnp.cos(angle)
        + 0.14128 * jnp.cos(2.0 * angle)
        - 0.01168 * jnp.cos(3.0 * angle)
    )


def make_tables():
    index = jnp.arange(NF, dtype=jnp.int32)
    phase = index[:, None] * index[None, :] % NF
    angle = phase.astype(jnp.float32) * (2.0 * math.pi / NF)
    return (jnp.cos(angle), jnp.sin(angle))


def delay_spectra(visibilities, flags):
    count = visibilities.shape[1]
    keep = (
        jnp.broadcast_to(flags[:, :, None], (count, NF // CB, CB))
        .reshape(count, NF)
        .astype(jnp.float32)
    )
    weight = keep * make_taper()[None, :]
    tapered = visibilities * weight[None, :, None, :]
    real_rows = tapered[0].reshape(count * NT, NF)
    imag_rows = tapered[1].reshape(count * NT, NF)
    cosine, sine = make_tables()
    high = lax.Precision.HIGHEST
    scale = 1.0 / math.sqrt(NF)
    real_out = (
        jnp.dot(real_rows, cosine, precision=high) + jnp.dot(imag_rows, sine, precision=high)
    ) * scale
    imag_out = (
        jnp.dot(imag_rows, cosine, precision=high) - jnp.dot(real_rows, sine, precision=high)
    ) * scale
    stacked = jnp.stack([real_out.reshape(count, NT, NF), imag_out.reshape(count, NT, NF)], 2)
    stacked = stacked.reshape(count, NT, 2, NF // BW, BW).transpose(3, 0, 1, 2, 4)
    return stacked.reshape(NF // BW, count, NT * 2 * BW).astype(jnp.bfloat16)


def shards(visibilities, flags):
    own = delay_spectra(visibilities, flags)
    bands, rows, inner = own.shape
    total = rows * lax.axis_size("bl")
    term = (
        jnp.einsum(
            "kbj,kcj->kbc",
            own,
            lax.all_gather(own, "bl", axis=1, tiled=True),
            preferred_element_type=jnp.float32,
        )
        / NT
    )
    own_wide = own.astype(jnp.float32)
    self_power = jnp.sum(own_wide * own_wide, axis=2) / NT
    partial_sum = jnp.sum(term, axis=(1, 2)) - jnp.sum(self_power, axis=1)
    bandpower = taken_together(partial_sum, "bl") / total
    return (term, bandpower)


def solution(mesh):
    return jax.shard_map(
        shards,
        mesh=mesh,
        in_specs=(P(None, ("group", "bl"), None, None), P(("group", "bl"), None)),
        out_specs=(P(None, ("group", "bl"), None), P("group")),
        check_vma=False,
    )
```

profile of v0, /device:TPU:0, one launch (start us, length us, event | category | flops | bytes accessed | tf_op | source)
XLA Modules:
  0.0 420.4 jit_solution(16420377505746367192)
XLA Ops:
  7.2 0.0 all-gather.2.cloned.1.call-start
  7.2 0.1 multiply_subtract_fusion
  7.3 0.7 convert_element_type.43
  8.0 0.1 copy.8
  8.0 0.1 broadcast_in_dim.4
  8.1 1.8 broadcast_multiply_fusion
  10.0 0.2 fusion.45
  10.2 20.0 %fusion.8 = f32[256,1024]{1,0:T(8,128)S(1)} fusion(f32[256,1024]{1,0:T(8,128)S(1)} %bitcast.14), kind=kOutput, calls=%fused_computation.13 | convolution fusion | flops 3235905536 | bytes 2097152 | tf_op jit(solution)/shard_map/dot_general | solution.py:57
  30.2 20.0 %fusion.10 = f32[256,1024]{1,0:T(8,128)S(1)} fusion(f32[256,1024]{1,0:T(8,128)S(1)} %bitcast.16), kind=kOutput, calls=%fused_computation.14 | convolution fusion | flops 3235905536 | bytes 2097152 | tf_op jit(solution)/shard_map/dot_general | solution.py:54
  50.2 19.7 %fusion.22 = bf16[256,1024]{1,0:T(8,128)(2,1)S(1)} fusion(f32[256,1024]{1,0:T(8,128)S(1)} %fusion.8, f32[256,1024]{1,0:T(8,128)S(1)} %bitcast.17), kind=kOutput, calls=%fused_computation.19 | convolution fusion | flops 3236691968 | bytes 2621440 | tf_op jit(solution)/shard_map/dot_general | solution.py:57
  70.0 19.5 %fusion.25 = bf16[256,1024]{1,0:T(8,128)(2,1)S(1)} fusion(f32[256,1024]{1,0:T(8,128)S(1)} %fusion.10, f32[256,1024]{1,0:T(8,128)S(1)} %bitcast.15), kind=kOutput, calls=%fused_computation.20 | convolution fusion | flops 3236691968 | bytes 2621440 | tf_op jit(solution)/shard_map/dot_general | solution.py:54
  89.5 1.6 stack.7
  91.1 2.6 stack.8
  93.7 4.5 %fusion.28 = bf16[32,16,16,2,32]{4,0,2,1,3:T(8,128)(2,1)} fusion(bf16[16,16,1,32,32]{4,3,1,0,2:T(8,128)(2,1)} %stack.8, bf16[16,16,1,32,32]{4,3,1,0,2:T(8,128)(2,1)S(1)} %stack.7), kind=kLoop, calls=%fused_computation.23 | loop fusion | flops 524288 | bytes 2097152 | tf_op jit(solution)/shard_map/convert_element_type | solution.py:61
  98.1 8.5 %copy.9 = bf16[32,16,16,2,32]{4,3,2,1,0:T(2,128)(2,1)} copy(bf16[32,16,16,2,32]{4,0,2,1,3:T(8,128)(2,1)} %fusion.28) | data formatting | bytes 2097152 | tf_op jit(solution)/shard_map/convert_element_type | solution.py:61
  106.6 11.7 %convert_element_type.49 = bf16[32,16,1024]{2,1,0:T(8,128)(2,1)} reshape(bf16[32,16,16,2,32]{4,3,2,1,0:T(2,128)(2,1)} %copy.9) | data formatting | bytes 2097152 | tf_op jit(solution)/shard_map/convert_element_type | solution.py:61
  118.4 0.0 copy-start
  118.4 0.0 all-gather.2.cloned.1.call-update
  118.4 2.8 multiply_reduce_fusion
  121.3 261.1 %all-gather.2.cloned.1.call-done = bf16[32,512,1024]{2,1,0:T(8,128)(2,1)} async-done(((bf16[32,16,1024]{2,1,0:T(8,128)(2,1)}), bf16[32,512,1024]{2,1,0:T(8,128)(2,1)}) %all-gather.2.cloned.1.call-update) | async-done | bytes 33554448 | tf_op jit(solution)/shard_map/all_gather | solution.py:72
  382.4 0.0 copy-done
  382.4 15.3 %fusion.46 = (f32[32]{0:T(128)S(1)}, f32[32,16,512]{2,1,0:T(8,128)}) fusion(bf16[32,16,1024]{2,1,0:T(8,128)(2,1)S(1)} %copy-done, bf16[32,512,1024]{2,1,0:T(8,128)(2,1)} %all-gather.2.cloned.1.call-done), kind=kOutput, calls=%fused_computation.45 | convolution fusion | flops 537395200 | bytes 35651712 | tf_op jit(solution)/shard_map/kbj,kcj->kbc/dot_general | solution.py:69
  397.7 15.3 %all_to_all.6 = f32[32,1,32]{2,1,0:T(1,128)S(1)} all-to-all(f32[32,1,32]{2,1,0:T(1,128)S(1)} %broadcast_in_dim.5), channel_id=1, replica_groups=mesh['group'=4,'bl'=32] {'bl'}, dimensions={0} | all-to-all | bytes 8192 | tf_op jit(solution)/shard_map/all_to_all | solution.py:15
  413.0 0.5 broadcast_multiply_fusion.1
  (5 shorter events, 0.1 us)
Async XLA Ops:
  7.2 375.2 %all-gather.2.cloned.1.call-start = ((), (), s32[]{:S(2)}) async-start(), calls=%async_computation.1 | async-start | bytes 34603008 | tf_op jit(solution)/shard_map/all_gather | solution.py:72
  118.4 264.0 %copy-start = (bf16[32,16,1024]{2,1,0:T(8,128)(2,1)S(1)}, bf16[32,16,1024]{2,1,0:T(8,128)(2,1)}, u32[]{:S(2)}) copy-start(bf16[32,16,1024]{2,1,0:T(8,128)(2,1)} %convert_element_type.49) | copy-start | bytes 3145732
Sparse Core Ops, SparseCore 0:
  118.5 263.7 all-gather.1
where the time goes:
time: 421 us; the launch traced here: 420 us
  waiting for transfers between devices  261 us (62%)
  matrix products  94.6 us (22%)
  local copies, waits for them, and re-layouts  24.8 us (6%)
  blocking collectives  15.3 us (4%)
  between operations  14.1 us (3%)
  other arithmetic  10.5 us (2%)
    all_gather x1, waiting for transfers between devices, shards(): lax.all_gather(own, 'bl', axis=1, tiled=True)  261 us
    convert_element_type x2, local copies, waits for them, and re-layouts, delay_spectra(): return stacked.reshape(NF // BW, count, NT * 2 * BW).astype(jnp.bfloat16)  20.2 us
    dot_general x1, matrix products, delay_spectra(): jnp.dot(imag_rows, cosine, precision=high)  20 us
    dot_general x1, matrix products, delay_spectra(): jnp.dot(real_rows, cosine, precision=high)  20 us
    dot_general x1, matrix products, delay_spectra(): jnp.dot(real_rows, sine, precision=high)  19.7 us
    dot_general x1, matrix products, delay_spectra(): jnp.dot(imag_rows, sine, precision=high)  19.5 us
    all_to_all x1, blocking collectives, copy_for_each(): return lax.all_to_all(copies, axis, split_axis=0, concat_axis=0, tiled=True)  15.3 us
    dot_general x1, matrix products, shards(): jnp.einsum('kbj,kcj->kbc', own, lax.all_gather(own, 'bl', axis=1, tiled=T...  15.3 us
  transfers between devices with their start and end apart: 1, of which 1 were waited for; matrix products, arithmetic and copies ran while one was open for 1% of the time, Pallas kernels for 0%

commit v1 on v0

--- a/solution.py
+++ b/solution.py
@@ -69,7 +69,9 @@
         jnp.einsum(
             "kbj,kcj->kbc",
             own,
-            lax.all_gather(own, "bl", axis=1, tiled=True),
+            jnp.concatenate(
+                lax.all_to_all(jnp.stack([own] * lax.axis_size("bl")), "bl", 0, 0), axis=1
+            ),
             preferred_element_type=jnp.float32,
         )
         / NT

time: 421 us -> 776 us (1.84)
  waiting for transfers between devices: 261 us -> 525 us
  blocking collectives: 15.3 us -> 71.6 us
  local copies, waits for them, and re-layouts: 24.8 us -> 58 us
  between operations: 14.1 us -> 0.72 us
  starting transfers between devices: 0.04 us -> 11.3 us
    all_to_all x0 -> x1, waiting for transfers between devices: none -> 525 us  [shards(): lax.all_to_all(jnp.stack([own] * lax.axis_size('bl')), 'bl', 0, 0)]
    all_gather x1 -> x0, waiting for transfers between devices: 261 us -> none  [shards(): lax.all_gather(own, 'bl', axis=1, tiled=True)]
    all_to_all x1, blocking collectives: 15.3 us -> 71.6 us  [copy_for_each(): return lax.all_to_all(copies, axis, split_axis=0, concat_axis=0, tiled=True)]
    reshape x0 -> x1, local copies, waits for them, and re-layouts: none -> 22.8 us  [shards(): jnp.concatenate(lax.all_to_all(jnp.stack([own] * lax.axis_size('bl')), 'b...]
    all_to_all x0 -> x1, starting transfers between devices: none -> 11.3 us  [shards(): lax.all_to_all(jnp.stack([own] * lax.axis_size('bl')), 'bl', 0, 0)]
    another operation x0 -> x1, local copies, waits for them, and re-layouts: none -> 11 us  [shards(): jnp.stack([own] * lax.axis_size('bl'))]
  transfers between devices with their start and end apart: 1 -> 1, of which waited for: 1 -> 1; matrix products, arithmetic and copies ran while one was open for 1% -> 0% of each run, Pallas kernels for 0% -> 0%
where the time goes in v1:
time: 776 us; the launch traced here: 771 us
  waiting for transfers between devices  525 us (68%)
  matrix products  94.6 us (12%)
  blocking collectives  71.6 us (9%)
  local copies, waits for them, and re-layouts  58 us (7%)
  starting transfers between devices  11.3 us (1%)
  other arithmetic  10.4 us (1%)
    all_to_all x1, waiting for transfers between devices, shards(): lax.all_to_all(jnp.stack([own] * lax.axis_size('bl')), 'bl', 0, 0)  525 us
    all_to_all x1, blocking collectives, copy_for_each(): return lax.all_to_all(copies, axis, split_axis=0, concat_axis=0, tiled=True)  71.6 us
    reshape x1, local copies, waits for them, and re-layouts, shards(): jnp.concatenate(lax.all_to_all(jnp.stack([own] * lax.axis_size('bl')), 'b...  22.8 us
    dot_general x1, matrix products, delay_spectra(): jnp.dot(real_rows, cosine, precision=high)  20 us
    dot_general x1, matrix products, delay_spectra(): jnp.dot(imag_rows, cosine, precision=high)  20 us
    dot_general x1, matrix products, delay_spectra(): jnp.dot(real_rows, sine, precision=high)  19.7 us
    dot_general x1, matrix products, delay_spectra(): jnp.dot(imag_rows, sine, precision=high)  19.5 us
    convert_element_type x2, local copies, waits for them, and re-layouts, delay_spectra(): return stacked.reshape(NF // BW, count, NT * 2 * BW).astype(jnp.bfloat16)  19.5 us
  transfers between devices with their start and end apart: 1, of which 1 were waited for; matrix products, arithmetic and copies ran while one was open for 0% of the time, Pallas kernels for 0%

profile of v1, /device:TPU:0, one launch (start us, length us, event | category | flops | bytes accessed | tf_op | source)
XLA Modules:
  0.0 771.0 jit_solution(12388866490129085089)
XLA Ops:
  0.6 0.1 multiply_subtract_fusion
  0.7 0.7 convert_element_type.45
  1.4 0.1 copy.12
  1.5 0.1 broadcast_in_dim.4
  1.6 1.8 broadcast_multiply_fusion
  3.4 0.2 fusion.45
  3.6 20.0 %fusion.8 = f32[256,1024]{1,0:T(8,128)S(1)} fusion(f32[256,1024]{1,0:T(8,128)S(1)} %bitcast.17), kind=kOutput, calls=%fused_computation.13 | convolution fusion | flops 3235905536 | bytes 2097152 | tf_op jit(solution)/shard_map/dot_general | solution.py:57
  23.6 20.0 %fusion.10 = f32[256,1024]{1,0:T(8,128)S(1)} fusion(f32[256,1024]{1,0:T(8,128)S(1)} %bitcast.19), kind=kOutput, calls=%fused_computation.14 | convolution fusion | flops 3235905536 | bytes 2097152 | tf_op jit(solution)/shard_map/dot_general | solution.py:54
  43.6 19.7 %fusion.22 = bf16[256,1024]{1,0:T(8,128)(2,1)S(1)} fusion(f32[256,1024]{1,0:T(8,128)S(1)} %fusion.8, f32[256,1024]{1,0:T(8,128)S(1)} %bitcast.20), kind=kOutput, calls=%fused_computation.19 | convolution fusion | flops 3236691968 | bytes 2621440 | tf_op jit(solution)/shard_map/dot_general | solution.py:57
  63.4 19.5 %fusion.25 = bf16[256,1024]{1,0:T(8,128)(2,1)S(1)} fusion(f32[256,1024]{1,0:T(8,128)S(1)} %fusion.10, f32[256,1024]{1,0:T(8,128)S(1)} %bitcast.18), kind=kOutput, calls=%fused_computation.20 | convolution fusion | flops 3236691968 | bytes 2621440 | tf_op jit(solution)/shard_map/dot_general | solution.py:54
  82.9 1.6 stack.8
  84.5 2.6 stack.9
  87.1 4.5 fusion.28
  91.6 8.5 %copy.13 = bf16[32,16,16,2,32]{4,3,2,1,0:T(2,128)(2,1)} copy(bf16[32,16,16,2,32]{4,0,2,1,3:T(8,128)(2,1)} %fusion.28) | data formatting | bytes 2097152 | tf_op jit(solution)/shard_map/convert_element_type | solution.py:61
  100.1 11.0 %convert_element_type.51 = bf16[32,16,1024]{2,1,0:T(8,128)(2,1)S(1)} reshape(bf16[32,16,16,2,32]{4,3,2,1,0:T(2,128)(2,1)} %copy.13) | data formatting | bytes 2097152 | tf_op jit(solution)/shard_map/convert_element_type | solution.py:61
  111.1 11.0 %stack.11 = bf16[32,32,16,1024]{3,2,1,0:T(8,128)(2,1)} broadcast(bf16[32,16,1024]{2,1,0:T(8,128)(2,1)S(1)} %convert_element_type.51), dimensions={1,2,3} | broadcast | bytes 34603008 | tf_op jit(solution)/shard_map/stack | solution.py:73
  122.1 11.3 %all-to-all-start = ((bf16[32,32,16,1024]{3,2,1,0:T(8,128)(2,1)}), bf16[32,32,16,1024]{3,2,1,0:T(8,128)(2,1)}, u32[]{:S(2)}, u32[]{:S(2)}) async-start(bf16[32,32,16,1024]{3,2,1,0:T(8,128)(2,1)} %stack.11), calls=%async_computation | async-start | bytes 67108864 | tf_op jit(solution)/shard_map/all_to_all | solution.py:73
  133.4 2.8 multiply_reduce_fusion
  136.2 524.6 %all-to-all-done = bf16[32,32,16,1024]{3,2,1,0:T(8,128)(2,1)} async-done(((bf16[32,32,16,1024]{3,2,1,0:T(8,128)(2,1)}), bf16[32,32,16,1024]{3,2,1,0:T(8,128)(2,1)}, u32[]{:S(2)}, u32[]{:S(2)}) %all-to-all-start) | async-done | bytes 33554464 | tf_op jit(solution)/shard_map/all_to_all | solution.py:73
  660.8 22.8 %copy.14 = bf16[32,32,16,1024]{3,2,1,0:T(8,128)(2,1)} copy(bf16[32,32,16,1024]{3,2,0,1:T(8,128)(2,1)} %bitcast.3) | data formatting | bytes 67108864 | tf_op jit(solution)/shard_map/reshape | solution.py:72
  683.6 15.3 %fusion.46 = (f32[32]{0:T(128)S(1)}, f32[32,16,512]{2,1,0:T(8,128)}) fusion(bf16[32,16,1024]{2,1,0:T(8,128)(2,1)S(1)} %convert_element_type.51, bf16[32,512,1024]{2,1,0:T(8,128)(2,1)} %bitcast.16), kind=kOutput, calls=%fused_computation.45 | convolution fusion | flops 537395200 | bytes 35651712 | tf_op jit(solution)/shard_map/kbj,kcj->kbc/dot_general | solution.py:69
  698.9 71.6 %all_to_all.11 = f32[32,1,32]{2,1,0:T(1,128)S(1)} all-to-all(f32[32,1,32]{2,1,0:T(1,128)S(1)} %broadcast_in_dim.5), channel_id=1, replica_groups=mesh['group'=4,'bl'=32] {'bl'}, dimensions={0} | all-to-all | bytes 8192 | tf_op jit(solution)/shard_map/all_to_all | solution.py:15
  770.5 0.5 broadcast_multiply_fusion.1
  (5 shorter events, 0.1 us)
Async XLA Ops:
  122.1 538.7 %all-to-all-start = ((bf16[32,32,16,1024]{3,2,1,0:T(8,128)(2,1)}), bf16[32,32,16,1024]{3,2,1,0:T(8,128)(2,1)}, u32[]{:S(2)}, u32[]{:S(2)}) async-start(bf16[32,32,16,1024]{3,2,1,0:T(8,128)(2,1)} %stack.11), calls=%async_computation | async-start | bytes 67108864 | tf_op jit(solution)/shard_map/all_to_all | solution.py:73
